TPU v7x, 32 devices: a whole 2x2x4 slice. The times are simulated.
32 devices in a mesh: cfg: 2 (over x), seq: 8 (over z, y), dp: 2 (over core).
Axes of the slice: x: 2, y: 2, z: 4, core: 2. Of those that a mesh axis runs over, the one named last changes fastest.
Arguments:
- teacher_query: bfloat16 [2, 2, 2, 1024, 2048], P('cfg', None, 'dp', 'seq'), may hold values from -6 to 6
- teacher_key: bfloat16 [2, 2, 2, 1024, 2048], P('cfg', None, 'dp', 'seq'), may hold values from -6 to 6
- teacher_value: bfloat16 [2, 2, 2, 1024, 2048], P('cfg', None, 'dp', 'seq'), may hold values from -6 to 6
- hidden: bfloat16 [2, 2, 1024, 3072], P('cfg', 'dp', 'seq'), may hold values from -6 to 6
- adapter_down_weight: bfloat16 [3, 3072, 128], replicated, may hold values from -0.109375 to 0.109375
- adapter_up_weight: bfloat16 [3, 128, 2048], replicated, may hold values from -0.5 to 0.5
- guidance_index: int32 [2, 2], P(None, 'dp'), may hold values from 0 to 7
- timestep_index: int32 [2, 2], P(None, 'dp'), may hold values from 0 to 999
Outputs:
- student_out: bfloat16 [2, 2, 1024, 2048], P('cfg', 'dp', 'seq')
- grad_down: float32 [3, 3072, 128], P(None, ('cfg', 'seq', 'dp'))
- grad_up: float32 [3, 128, 2048], P(None, ('cfg', 'dp'), 'seq')
All inputs are finite; a program needn't handle non-finite values.
Results may differ from a plain program's by a relative error of at most 0.02.
The roundings to bfloat16 on the way count: a program that leaves them out, or rounds other values in their place, can miss the bound.
Values may be sent and summed in bfloat16 or wider, within the bound.
A program may use at most 128 MiB of HBM per device.

v0:
```python
import math
import jax
import jax.numpy as jnp
from jax import lax
from jax.sharding import PartitionSpec as P

HDIM = 128
ADAPTER_RANK = 128
TSTEPS = 1000


def passed_along(value, axis, steps):
    count = lax.axis_size(axis)
    leading, last = (max(0, -steps), min(count, count - steps))
    return lax.ppermute(value, axis, [(source, source + steps) for source in range(leading, last)])


def head_probs(query_block, key_heads, factor):
    scores = (
        jnp.einsum("qhd,khd->hqk", query_block, key_heads, preferred_element_type=jnp.float32)
        * factor
    )
    highest = jnp.max(scores, axis=-1, keepdims=True)
    raised = jnp.exp(scores - highest)
    return raised / jnp.sum(raised, axis=-1, keepdims=True)


def attention_forward(queries, keys, values):
    length, columns_all = queries.shape
    heads_here = columns_all // HDIM
    factor = HDIM ** (-0.5)
    step_rows = min(512, length)
    key_heads = keys.reshape(length, heads_here, HDIM)
    value_heads = values.reshape(length, heads_here, HDIM)
    query_blocks = queries.reshape(length // step_rows, step_rows, heads_here, HDIM)

    def one_block(query_block):
        weights = head_probs(query_block, key_heads, factor).astype(jnp.bfloat16)
        return jnp.einsum("hqk,khd->qhd", weights, value_heads, preferred_element_type=jnp.float32)

    return lax.map(one_block, query_blocks).reshape(length, columns_all)


def attention_backward(queries, keys, values, upstream):
    length, columns_all = queries.shape
    heads_here = columns_all // HDIM
    factor = HDIM ** (-0.5)
    step_rows = min(512, length)
    key_heads = keys.reshape(length, heads_here, HDIM)
    value_heads = values.reshape(length, heads_here, HDIM)
    query_blocks = queries.reshape(length // step_rows, step_rows, heads_here, HDIM)
    upstream_blocks = upstream.reshape(length // step_rows, step_rows, heads_here, HDIM)

    def one_block(running, block_pair):
        key_grad, value_grad = running
        query_block, upstream_block = block_pair
        probability = head_probs(query_block, key_heads, factor)
        weights = probability.astype(jnp.bfloat16)
        value_grad = value_grad + jnp.einsum(
            "hqk,qhd->khd", weights, upstream_block, preferred_element_type=jnp.float32
        )
        prob_grad = jnp.einsum(
            "qhd,khd->hqk", upstream_block, value_heads, preferred_element_type=jnp.float32
        )
        center = jnp.sum(probability * prob_grad, axis=-1, keepdims=True)
        score_grad = (probability * (prob_grad - center)).astype(jnp.bfloat16)
        query_grad = (
            jnp.einsum("hqk,khd->qhd", score_grad, key_heads, preferred_element_type=jnp.float32)
            * factor
        )
        key_grad = (
            key_grad
            + jnp.einsum(
                "hqk,qhd->khd", score_grad, query_block, preferred_element_type=jnp.float32
            )
            * factor
        )
        return ((key_grad, value_grad), query_grad)

    empty_grad = jnp.zeros((length, heads_here, HDIM), jnp.float32)
    (key_grad, value_grad), query_grad = lax.scan(
        one_block, (empty_grad, empty_grad), (query_blocks, upstream_blocks)
    )
    return (
        query_grad.reshape(length, columns_all).astype(jnp.bfloat16),
        key_grad.reshape(length, columns_all).astype(jnp.bfloat16),
        value_grad.reshape(length, columns_all).astype(jnp.bfloat16),
    )


def body(
    teacher_query,
    teacher_key,
    teacher_value,
    hidden,
    adapter_down_weight,
    adapter_up_weight,
    guidance_index,
    timestep_index,
):
    cfg_index = lax.axis_index("cfg")
    seq_count = lax.axis_size("seq")
    tok_here = hidden.shape[2]
    total_rows = 2 * lax.axis_size("dp") * tok_here * seq_count
    input_features = hidden[0, 0]
    half_cols = input_features.shape[1] // (2 * seq_count)
    split_view = input_features.reshape(tok_here, 2, seq_count, half_cols)
    column_block = lax.all_to_all(split_view, "seq", split_axis=2, concat_axis=0, tiled=True)
    column_block = column_block.reshape(tok_here * seq_count, 2 * half_cols)
    own_pass = (teacher_query[0, :, 0], teacher_key[0, :, 0], teacher_value[0, :, 0])
    teacher_heads = (
        lax.all_to_all(own_pass[0], "seq", split_axis=2, concat_axis=1, tiled=True),
        lax.all_to_all(own_pass[1], "seq", split_axis=2, concat_axis=1, tiled=True),
        lax.all_to_all(own_pass[2], "seq", split_axis=2, concat_axis=1, tiled=True),
    )
    teacher_local = jnp.stack(
        [
            attention_forward(
                teacher_heads[0][half_index],
                teacher_heads[1][half_index],
                teacher_heads[2][half_index],
            )
            for half_index in range(2)
        ]
    )
    teacher_tokens = lax.all_to_all(
        teacher_local.astype(jnp.bfloat16), "seq", split_axis=1, concat_axis=2, tiled=True
    )
    guide_scale = 1.0 + 0.5 * guidance_index[:, 0].astype(jnp.float32)
    time_frac = (timestep_index[:, 0].astype(jnp.float32) + 0.5) / TSTEPS
    own_scale = lax.dynamic_index_in_dim(guide_scale, cfg_index, 0, keepdims=False)
    own_time = lax.dynamic_index_in_dim(time_frac, cfg_index, 0, keepdims=False)
    weighting = jnp.where(cfg_index == 0, guide_scale, 1.0 - guide_scale)
    weighted = weighting[:, None, None] * teacher_tokens.astype(jnp.float32)
    target = lax.psum_scatter(
        weighted.astype(jnp.bfloat16), "cfg", scatter_dimension=0, tiled=True
    ).astype(jnp.float32)[0]
    rank_index = jnp.arange(1, ADAPTER_RANK + 1).astype(jnp.float32)
    feature_modulation = 1.0 + 0.5 * jnp.cos(
        math.pi * rank_index * own_time + 0.25 * rank_index * own_scale
    )
    rank_projected = (
        jnp.einsum(
            "cl,elj->ecj", input_features, adapter_down_weight, preferred_element_type=jnp.float32
        )
        * feature_modulation
    ).astype(jnp.bfloat16)
    partner = passed_along(
        (teacher_query[0, 1, 0], teacher_key[0, 1, 0], teacher_value[0, 1, 0]), "cfg", 1
    )
    projected = []
    for stack_member in range(3):
        frozen = jnp.where(cfg_index == 0, own_pass[stack_member][0], partner[stack_member])
        adapted_output = jnp.dot(
            rank_projected[stack_member],
            adapter_up_weight[stack_member],
            preferred_element_type=jnp.float32,
        )
        projected.append((frozen.astype(jnp.float32) + adapted_output).astype(jnp.bfloat16))
    student = (
        lax.all_to_all(projected[0], "seq", split_axis=1, concat_axis=0, tiled=True),
        lax.all_to_all(projected[1], "seq", split_axis=1, concat_axis=0, tiled=True),
        lax.all_to_all(projected[2], "seq", split_axis=1, concat_axis=0, tiled=True),
    )
    student_local = attention_forward(student[0], student[1], student[2]).astype(jnp.bfloat16)
    student_tokens = lax.all_to_all(student_local, "seq", split_axis=0, concat_axis=1, tiled=True)
    upstream = (
        (student_tokens.astype(jnp.float32) - target) * (1.0 / math.sqrt(total_rows))
    ).astype(jnp.bfloat16)
    upstream_heads = lax.all_to_all(upstream, "seq", split_axis=1, concat_axis=0, tiled=True)
    grads_heads = attention_backward(student[0], student[1], student[2], upstream_heads)
    grads_tokens = (
        lax.all_to_all(grads_heads[0], "seq", split_axis=0, concat_axis=1, tiled=True),
        lax.all_to_all(grads_heads[1], "seq", split_axis=0, concat_axis=1, tiled=True),
        lax.all_to_all(grads_heads[2], "seq", split_axis=0, concat_axis=1, tiled=True),
    )
    gradient_stack = jnp.stack(grads_tokens)
    rank_backward = jnp.einsum(
        "sli,smi->slm", gradient_stack, adapter_up_weight, preferred_element_type=jnp.float32
    )
    up_partial = jnp.einsum(
        "ktr,ktc->krc", rank_projected, gradient_stack, preferred_element_type=jnp.float32
    )
    per_seq = lax.psum_scatter(
        up_partial.astype(jnp.bfloat16), "seq", scatter_dimension=2, tiled=True
    )
    grad_up = lax.psum_scatter(per_seq, ("cfg", "dp"), scatter_dimension=1, tiled=True).astype(
        jnp.float32
    )
    low_grad = (rank_backward * feature_modulation).astype(jnp.bfloat16)
    grad_rows = lax.all_gather(low_grad, "seq", axis=1, tiled=True)
    column_partial = jnp.einsum(
        "tc,ktr->kcr", column_block, grad_rows, preferred_element_type=jnp.float32
    )
    grad_down = lax.psum_scatter(
        column_partial.astype(jnp.bfloat16), ("cfg", "dp"), scatter_dimension=1, tiled=True
    ).astype(jnp.float32)
    return (student_tokens[None, None], grad_down, grad_up)


def solution(mesh):
    placed = (
        P("cfg", None, "dp", "seq", None),
        P("cfg", None, "dp", "seq", None),
        P("cfg", None, "dp", "seq", None),
        P("cfg", "dp", "seq", None),
        P(),
        P(),
        P(None, "dp"),
        P(None, "dp"),
    )
    return jax.shard_map(
        body,
        mesh=mesh,
        in_specs=placed,
        out_specs=(
            P("cfg", "dp", "seq", None),
            P(None, ("cfg", "seq", "dp"), None),
            P(None, ("cfg", "dp"), "seq"),
        ),
        check_vma=False,
    )
```

profile of v0, /device:TPU:0, one launch (start us, length us, event | category | flops | bytes accessed | tf_op | source)
XLA Modules:
  0.0 490.0 jit_solution(14562616477603965680)
XLA Ops:
  11.0 7.3 %all-to-all-start.5 = ((bf16[2,128,2048]{1,0,2:T(2,128)(2,1)}), bf16[2,128,2048]{1,0,2:T(2,128)(2,1)}, u32[]{:S(2)}, u32[]{:S(2)}) async-start(bf16[2,128,2048]{1,0,2:T(2,128)(2,1)} %bitcast.305), calls=%async_computation.5 | async-start | bytes 2097152 | tf_op jit(solution)/shard_map/all_to_all | solution.py:113
  22.0 22.2 %all-to-all-done.5 = bf16[2,128,2048]{1,0,2:T(2,128)(2,1)} async-done(((bf16[2,128,2048]{1,0,2:T(2,128)(2,1)}), bf16[2,128,2048]{1,0,2:T(2,128)(2,1)}, u32[]{:S(2)}, u32[]{:S(2)}) %all-to-all-start.5) | async-done | bytes 1048608 | tf_op jit(solution)/shard_map/all_to_all | solution.py:113
  61.2 12.8 %all-to-all-done.6 = bf16[2,128,2048]{1,0,2:T(2,128)(2,1)} async-done(((bf16[2,128,2048]{1,0,2:T(2,128)(2,1)}), bf16[2,128,2048]{1,0,2:T(2,128)(2,1)}, u32[]{:S(2)}, u32[]{:S(2)}) %all-to-all-start.6) | async-done | bytes 1048608 | tf_op jit(solution)/shard_map/all_to_all | solution.py:114
  92.4 11.4 %all-to-all-done.4 = bf16[2,128,2048]{1,0,2:T(2,128)(2,1)} async-done(((bf16[2,128,2048]{1,0,2:T(2,128)(2,1)}), bf16[2,128,2048]{1,0,2:T(2,128)(2,1)}, u32[]{:S(2)}, u32[]{:S(2)}) %all-to-all-start.4) | async-done | bytes 1048608 | tf_op jit(solution)/shard_map/all_to_all | solution.py:112
  121.8 5.4 %all-to-all-start.2 = ((bf16[128,8,256]{0,2,1:T(8,128)(2,1)}), bf16[128,8,256]{0,2,1:T(8,128)(2,1)S(1)}, u32[]{:S(2)}, u32[]{:S(2)}) async-start(bf16[128,8,256]{0,2,1:T(8,128)(2,1)} %bitcast.28), calls=%async_computation.2 | async-start | bytes 1048576 | tf_op jit(solution)/shard_map/all_to_all | solution.py:163
  127.2 15.5 %while.46 = (s32[]{:T(128)}, bf16[2,512,2,128]{3,1,2,0:T(8,128)(2,1)S(1)}, bf16[2,512,2,128]{3,2,1,0:T(2,128)(2,1)S(1)}, bf16[1024,2,128]{2,0,1:T(8,128)(2,1)}, bf16[1024,2,128]{2,0,1:T(8,128)(2,1)}, /*index=5*/s32[]{:T(128)}) while((s32[]{:T(128)}, bf16[2,512,2,128]{3,1,2,0:T(8,128)(2,1)S(1)}, bf16[2,512,2,128]{3,2,1,0:T(2,128)(2,1)S(1)}, ...), condition=%wide.region_7.8_spmd, body=%wide.region_4.7_spmd.sunk | while | flops 542114816 | bytes 10756173 | solution.py:41
  135.2 4.4 fusion.182
  147.4 6.0 %all-to-all-start = ((bf16[128,8,256]{2,0,1:T(8,128)(2,1)}), bf16[128,8,256]{2,0,1:T(8,128)(2,1)S(1)}, u32[]{:S(2)}, u32[]{:S(2)}) async-start(bf16[128,8,256]{2,0,1:T(8,128)(2,1)} %bitcast.251), calls=%async_computation | async-start | bytes 1048576 | tf_op jit(solution)/shard_map/all_to_all | solution.py:161
  154.3 16.8 %while.47 = (s32[]{:T(128)}, bf16[2,512,2,128]{3,1,2,0:T(8,128)(2,1)}, bf16[2,512,2,128]{3,2,1,0:T(2,128)(2,1)S(1)}, bf16[1024,2,128]{2,0,1:T(8,128)(2,1)}, bf16[1024,2,128]{2,0,1:T(8,128)(2,1)}, /*index=5*/s32[]{:T(128)}) while((s32[]{:T(128)}, bf16[2,512,2,128]{3,1,2,0:T(8,128)(2,1)}, bf16[2,512,2,128]{3,2,1,0:T(2,128)(2,1)S(1)}, ...), condition=%wide.region_11.12_spmd, body=%wide.region_8.11_spmd.sunk | while | flops 542114816 | bytes 10756681 | solution.py:41
  179.5 6.0 %all-to-all-start.7 = ((bf16[2,1024,256]{2,0,1:T(2,128)(2,1)}), bf16[2,1024,256]{2,0,1:T(2,128)(2,1)S(1)}, u32[]{:S(2)}, u32[]{:S(2)}) async-start(bf16[2,1024,256]{2,0,1:T(2,128)(2,1)} %copy.116), calls=%async_computation.7 | async-start | bytes 2097152 | tf_op jit(solution)/shard_map/all_to_all | solution.py:126
  189.0 21.0 %all-to-all-done.7 = bf16[2,1024,256]{2,0,1:T(2,128)(2,1)S(1)} async-done(((bf16[2,1024,256]{2,0,1:T(2,128)(2,1)}), bf16[2,1024,256]{2,0,1:T(2,128)(2,1)S(1)}, u32[]{:S(2)}, u32[]{:S(2)}) %all-to-all-start.7) | async-done | bytes 1048608 | tf_op jit(solution)/shard_map/all_to_all | solution.py:126
  215.0 13.1 %while.45 = (s32[]{:T(128)}, bf16[2,512,2,128]{3,1,2,0:T(8,128)(2,1)S(1)}, bf16[2,512,2,128]{3,1,2,0:T(8,128)(2,1)S(1)}, bf16[1024,2,128]{2,0,1:T(8,128)(2,1)S(1)}, bf16[1024,2,128]{2,0,1:T(8,128)(2,1)}, /*index=5*/s32[]{:T(128)}) while((s32[]{:T(128)}, bf16[2,512,2,128]{3,1,2,0:T(8,128)(2,1)S(1)}, bf16[2,512,2,128]{3,1,2,0:T(8,128)(2,1)S(1)}, ...), condition=%wide.region_3.4_spmd, body=%wide.region_0.3_spmd.sunk | while | flops 542114816 | bytes 12329065 | solution.py:41
  235.7 11.8 %all-to-all-done.3 = bf16[8,128,256]{2,1,0:T(8,128)(2,1)S(1)} async-done(((bf16[8,128,256]{2,1,0:T(8,128)(2,1)}), bf16[8,128,256]{2,1,0:T(8,128)(2,1)S(1)}, u32[]{:S(2)}, u32[]{:S(2)}) %all-to-all-start.3) | async-done | bytes 524320 | tf_op jit(solution)/shard_map/all_to_all | solution.py:166
  252.3 14.4 %all-to-all-done.8 = bf16[128,8,256]{2,0,1:T(8,128)(2,1)S(1)} async-done(((bf16[128,8,256]{2,0,1:T(8,128)(2,1)}), bf16[128,8,256]{2,0,1:T(8,128)(2,1)S(1)}, u32[]{:S(2)}, u32[]{:S(2)}) %all-to-all-start.8) | async-done | bytes 524320 | tf_op jit(solution)/shard_map/all_to_all | solution.py:170
  267.7 31.3 %while.48 = (s32[]{:T(128)}, f32[1024,2,128]{0,2,1:T(8,128)S(1)}, f32[1024,2,128]{0,2,1:T(8,128)}, bf16[2,512,2,128]{3,1,2,0:T(8,128)(2,1)}, bf16[2,512,2,128]{3...) while((s32[]{:T(128)}, f32[1024,2,128]{0,2,1:T(8,128)S(1)}, ...), condition=%wide.region_17.18_spmd.clone, body=%wide.region_13.17_spmd.clone.sunk | while | flops 1356201984 | bytes 79193864 | solution.py:81
  267.7 4.6 fusion.196
  282.7 4.7 fusion.196
  306.7 13.4 %all-to-all-done.9 = bf16[8,128,256]{2,1,0:T(8,128)(2,1)S(1)} async-done(((bf16[8,128,256]{2,1,0:T(8,128)(2,1)}), bf16[8,128,256]{2,1,0:T(8,128)(2,1)S(1)}, u32[]{:S(2)}, u32[]{:S(2)}) %all-to-all-start.9) | async-done | bytes 524320 | tf_op jit(solution)/shard_map/all_to_all | solution.py:173
  326.2 12.1 %all-to-all-done.10 = bf16[8,128,256]{2,1,0:T(8,128)(2,1)S(1)} async-done(((bf16[8,128,256]{2,1,0:T(8,128)(2,1)}), bf16[8,128,256]{2,1,0:T(8,128)(2,1)S(1)}, u32[]{:S(2)}, u32[]{:S(2)}) %all-to-all-start.10) | async-done | bytes 524320 | tf_op jit(solution)/shard_map/all_to_all | solution.py:174
  343.2 13.5 %all-to-all-done.11 = bf16[8,128,256]{2,1,0:T(8,128)(2,1)S(1)} async-done(((bf16[8,128,256]{2,1,0:T(8,128)(2,1)}), bf16[8,128,256]{2,1,0:T(8,128)(2,1)S(1)}, u32[]{:S(2)}, u32[]{:S(2)}) %all-to-all-start.11) | async-done | bytes 524320 | tf_op jit(solution)/shard_map/all_to_all | solution.py:175
  362.6 36.0 %all_to_all.182 = bf16[128,2,8,192]{0,3,1,2:T(8,128)(2,1)S(1)} all-to-all(bf16[128,2,8,192]{0,3,1,2:T(8,128)(2,1)S(1)} %copy.131), channel_id=1, replica_groups=mesh['cfg'=2,'seq'=8,'dp'=2] {'seq'}, dimensions={2} | all-to-all | bytes 1572864 | tf_op jit(solution)/shard_map/all_to_all | solution.py:108
  402.9 32.7 %all_gather.3 = bf16[3,1024,128]{2,1,0:T(8,128)(2,1)S(1)} all-gather(bf16[3,128,128]{2,1,0:T(8,128)(2,1)S(1)} %fusion.92), channel_id=1, replica_groups=mesh['cfg'=2,'seq'=8,'dp'=2] {'seq'}, dimensions={1}, use_global_device_ids=true | all-gather | bytes 884736 | tf_op jit(solution)/shard_map/all_gather | solution.py:191
  442.0 17.9 %reduce-scatter.13.cloned.1.call-done = bf16[96,384]{1,0:T(8,128)(2,1)} async-done(((bf16[384,384]{1,0:T(8,128)(2,1)}), bf16[96,384]{1,0:T(8,128)(2,1)}) %reduce-scatter.13.cloned.1.call-update) | async-done | bytes 73744
  461.7 20.3 %reduce-scatter.11.cloned.1.call-done = bf16[3,32,256]{2,1,0:T(8,128)(2,1)} async-done(((bf16[3,128,256]{2,1,0:T(8,128)(2,1)}), bf16[3,32,256]{2,1,0:T(8,128)(2,1)}) %reduce-scatter.11.cloned.1.call-update) | async-done | bytes 49168 | tf_op jit(solution)/shard_map/reduce_scatter | solution.py:187
  (211 shorter events, 196.2 us)
Async XLA Ops:
  7.2 79.2 %copy-start = (bf16[3,3072,128]{2,1,0:T(8,128)(2,1)S(1)}, bf16[3,3072,128]{2,1,0:T(8,128)(2,1)}, u32[]{:S(2)}) copy-start(bf16[3,3072,128]{2,1,0:T(8,128)(2,1)} %param.20) | copy-start | bytes 7077892
  7.2 41.3 %copy-start.10 = (bf16[1,2,1,128,2048]{4,3,2,1,0:T(8,128)(2,1)S(1)}, bf16[1,2,1,128,2048]{4,3,2,1,0:T(8,128)(2,1)}, u32[]{:S(2)}) copy-start(bf16[1,2,1,128,2048]{4,3,2,1,0:T(8,128)(2,1)} %param.17) | copy-start | bytes 3145732
  11.0 33.2 %all-to-all-start.5 = ((bf16[2,128,2048]{1,0,2:T(2,128)(2,1)}), bf16[2,128,2048]{1,0,2:T(2,128)(2,1)}, u32[]{:S(2)}, u32[]{:S(2)}) async-start(bf16[2,128,2048]{1,0,2:T(2,128)(2,1)} %bitcast.305), calls=%async_computation.5 | async-start | bytes 2097152 | tf_op jit(solution)/shard_map/all_to_all | solution.py:113
  44.2 29.8 %all-to-all-start.6 = ((bf16[2,128,2048]{1,0,2:T(2,128)(2,1)}), bf16[2,128,2048]{1,0,2:T(2,128)(2,1)}, u32[]{:S(2)}, u32[]{:S(2)}) async-start(bf16[2,128,2048]{1,0,2:T(2,128)(2,1)} %bitcast.304), calls=%async_computation.6 | async-start | bytes 2097152 | tf_op jit(solution)/shard_map/all_to_all | solution.py:114
  49.3 39.0 %collective-permute-start.1 = (bf16[128,2048]{1,0:T(8,128)(2,1)}, bf16[128,2048]{1,0:T(8,128)(2,1)}, u32[]{:S(2)}, u32[]{:S(2)}) collective-permute-start(bf16[128,2048]{1,0:T(8,128)(2,1)} %slice_bitcast_fusion.1), channel_id=1, source_target_pairs={{0,16},{1,17},{2,18},{3,19},{4,20},{5,21},{6,22},{7,23},{8,24},{9,... | collective-permute-start | bytes 1572872 | tf_op jit(solution)/shard_map/ppermute | solution.py:15
  55.4 35.4 %collective-permute-start.2 = (bf16[128,2048]{1,0:T(8,128)(2,1)}, bf16[128,2048]{1,0:T(8,128)(2,1)}, u32[]{:S(2)}, u32[]{:S(2)}) collective-permute-start(bf16[128,2048]{1,0:T(8,128)(2,1)} %slice_bitcast_fusion), channel_id=1, source_target_pairs={{0,16},{1,17},{2,18},{3,19},{4,20},{5,21},{6,22},{7,23},{8,24},{9,... | collective-permute-start | bytes 1572872 | tf_op jit(solution)/shard_map/ppermute | solution.py:15
  74.0 29.7 %all-to-all-start.4 = ((bf16[2,128,2048]{1,0,2:T(2,128)(2,1)}), bf16[2,128,2048]{1,0,2:T(2,128)(2,1)}, u32[]{:S(2)}, u32[]{:S(2)}) async-start(bf16[2,128,2048]{1,0,2:T(2,128)(2,1)} %bitcast.303), calls=%async_computation.4 | async-start | bytes 2097152 | tf_op jit(solution)/shard_map/all_to_all | solution.py:112
  80.2 27.0 %collective-permute-start = (bf16[128,2048]{1,0:T(8,128)(2,1)}, bf16[128,2048]{1,0:T(8,128)(2,1)}, u32[]{:S(2)}, u32[]{:S(2)}) collective-permute-start(bf16[128,2048]{1,0:T(8,128)(2,1)} %slice_bitcast_fusion.2), channel_id=1, source_target_pairs={{0,16},{1,17},{2,18},{3,19},{4,20},{5,21},{6,22},{7,23},{8,24},{9,... | collective-permute-start | bytes 1572872 | tf_op jit(solution)/shard_map/ppermute | solution.py:15
  103.7 18.0 %all-to-all-start.1 = ((bf16[128,8,256]{0,2,1:T(8,128)(2,1)}), bf16[128,8,256]{0,2,1:T(8,128)(2,1)S(1)}, u32[]{:S(2)}, u32[]{:S(2)}) async-start(bf16[128,8,256]{0,2,1:T(8,128)(2,1)} %bitcast.22), calls=%async_computation.1 | async-start | bytes 1048576 | tf_op jit(solution)/shard_map/all_to_all | solution.py:162
  121.8 25.6 %all-to-all-start.2 = ((bf16[128,8,256]{0,2,1:T(8,128)(2,1)}), bf16[128,8,256]{0,2,1:T(8,128)(2,1)S(1)}, u32[]{:S(2)}, u32[]{:S(2)}) async-start(bf16[128,8,256]{0,2,1:T(8,128)(2,1)} %bitcast.28), calls=%async_computation.2 | async-start | bytes 1048576 | tf_op jit(solution)/shard_map/all_to_all | solution.py:163
  147.4 31.4 %all-to-all-start = ((bf16[128,8,256]{2,0,1:T(8,128)(2,1)}), bf16[128,8,256]{2,0,1:T(8,128)(2,1)S(1)}, u32[]{:S(2)}, u32[]{:S(2)}) async-start(bf16[128,8,256]{2,0,1:T(8,128)(2,1)} %bitcast.251), calls=%async_computation | async-start | bytes 1048576 | tf_op jit(solution)/shard_map/all_to_all | solution.py:161
  179.5 30.4 %all-to-all-start.7 = ((bf16[2,1024,256]{2,0,1:T(2,128)(2,1)}), bf16[2,1024,256]{2,0,1:T(2,128)(2,1)S(1)}, u32[]{:S(2)}, u32[]{:S(2)}) async-start(bf16[2,1024,256]{2,0,1:T(2,128)(2,1)} %copy.116), calls=%async_computation.7 | async-start | bytes 2097152 | tf_op jit(solution)/shard_map/all_to_all | solution.py:126
  185.5 48.9 %reduce-scatter.7.cloned.1.call-start = ((), (), s32[]{:S(2)}) async-start(), calls=%async_computation.17 | async-start | bytes 1572864 | tf_op jit(solution)/shard_map/reduce_scatter | solution.py:135
  228.7 39.0 %copy-start.19 = (bf16[1024,2,128]{2,0,1:T(8,128)(2,1)S(1)}, bf16[1024,2,128]{2,0,1:T(8,128)(2,1)}, u32[]{:S(2)}) copy-start(bf16[1024,2,128]{2,0,1:T(8,128)(2,1)} %get-tuple-element.580) | copy-start | bytes 1572868
  229.9 17.7 %all-to-all-start.3 = ((bf16[8,128,256]{2,1,0:T(8,128)(2,1)}), bf16[8,128,256]{2,1,0:T(8,128)(2,1)S(1)}, u32[]{:S(2)}, u32[]{:S(2)}) async-start(bf16[8,128,256]{2,1,0:T(8,128)(2,1)} %convert_element_type.143), calls=%async_computation.3 | async-start | bytes 1048576 | tf_op jit(solution)/shard_map/all_to_all | solution.py:166
  248.5 18.1 %all-to-all-start.8 = ((bf16[128,8,256]{2,0,1:T(8,128)(2,1)}), bf16[128,8,256]{2,0,1:T(8,128)(2,1)S(1)}, u32[]{:S(2)}, u32[]{:S(2)}) async-start(bf16[128,8,256]{2,0,1:T(8,128)(2,1)} %multiply_convert_fusion.1), calls=%async_computation.9 | async-start | bytes 1048576 | tf_op jit(solution)/shard_map/all_to_all | solution.py:170
  301.7 18.3 %all-to-all-start.9 = ((bf16[8,128,256]{2,1,0:T(8,128)(2,1)}), bf16[8,128,256]{2,1,0:T(8,128)(2,1)S(1)}, u32[]{:S(2)}, u32[]{:S(2)}) async-start(bf16[8,128,256]{2,1,0:T(8,128)(2,1)} %convert_element_type.152), calls=%async_computation.10 | async-start | bytes 1048576 | tf_op jit(solution)/shard_map/all_to_all | solution.py:173
  320.0 18.3 %all-to-all-start.10 = ((bf16[8,128,256]{2,1,0:T(8,128)(2,1)}), bf16[8,128,256]{2,1,0:T(8,128)(2,1)S(1)}, u32[]{:S(2)}, u32[]{:S(2)}) async-start(bf16[8,128,256]{2,1,0:T(8,128)(2,1)} %copy.144), calls=%async_computation.11 | async-start | bytes 1048576 | tf_op jit(solution)/shard_map/all_to_all | solution.py:174
  338.3 18.3 %all-to-all-start.11 = ((bf16[8,128,256]{2,1,0:T(8,128)(2,1)}), bf16[8,128,256]{2,1,0:T(8,128)(2,1)S(1)}, u32[]{:S(2)}, u32[]{:S(2)}) async-start(bf16[8,128,256]{2,1,0:T(8,128)(2,1)} %copy.145), calls=%async_computation.12 | async-start | bytes 1048576 | tf_op jit(solution)/shard_map/all_to_all | solution.py:175
  342.0 98.2 %reduce-scatter.9.cloned.1.call-start = ((), (), s32[]{:S(2)}) async-start(), calls=%async_computation.18 | async-start | bytes 1769472 | tf_op jit(solution)/shard_map/reduce_scatter | solution.py:184
  362.1 97.8 %reduce-scatter.13.cloned.1.call-start = ((), (), s32[]{:S(2)}) async-start(), calls=%async_computation.20 | async-start | bytes 368640
  400.3 40.4 %copy-start.9 = (bf16[8,128,256]{2,1,0:T(8,128)(2,1)S(1)}, bf16[8,128,256]{2,1,0:T(8,128)(2,1)}, u32[]{:S(2)}) copy-start(bf16[8,128,256]{2,1,0:T(8,128)(2,1)} %copy-done.8) | copy-start | bytes 1572868
  400.3 83.1 %copy-start.1 = (bf16[3,3072,128]{2,1,0:T(8,128)(2,1)S(1)}, bf16[3,3072,128]{2,1,0:T(8,128)(2,1)}, u32[]{:S(2)}) copy-start(bf16[3,3072,128]{2,1,0:T(8,128)(2,1)} %param.20) | copy-start | bytes 7077892
  440.1 41.9 %reduce-scatter.11.cloned.1.call-start = ((), (), s32[]{:S(2)}) async-start(), calls=%async_computation.19 | async-start | bytes 245760 | tf_op jit(solution)/shard_map/reduce_scatter | solution.py:187
  (26 other events, 269.5 us)
Sparse Core Ops, SparseCore 0:
  215.1 19.3 reduce-scatter.6
  362.2 74.5 reduce-scatter.8
  440.2 19.5 reduce-scatter.12
  462.2 19.7 reduce-scatter.10
where the time goes:
time: 493 us; the launch traced here: 490 us
  waiting for transfers between devices  173 us (35%)
  matrix products  86.5 us (18%)
  local copies, waits for them, and re-layouts  70.6 us (14%)
  blocking collectives  68.7 us (14%)
  starting transfers between devices  65.5 us (13%)
  between operations  15.7 us (3%)
  other arithmetic  9.88 us (2%)
    all_to_all x1, blocking collectives, body(): lax.all_to_all(split_view, 'seq', split_axis=2, concat_axis=0, tiled=True)  36 us
    sub x8, matrix products, head_probs(): raised = jnp.exp(scores - highest)  33.6 us
    all_gather x1, blocking collectives, body(): grad_rows = lax.all_gather(low_grad, 'seq', axis=1, tiled=True)  32.7 us
    all_to_all x1, waiting for transfers between devices, body(): lax.all_to_all(own_pass[1], 'seq', split_axis=2, concat_axis=1, tiled=True)  22.2 us
    all_to_all x1, waiting for transfers between devices, body(): lax.all_to_all(teacher_local.astype(jnp.bfloat16), 'seq', split_axis=1, c...  21 us
    reduce_scatter x1, waiting for transfers between devices, body(): lax.psum_scatter(per_seq, ('cfg', 'dp'), scatter_dimension=1, tiled=True)  20.3 us
    dot_general x6, matrix products, one_block(): jnp.einsum('hqk,khd->qhd', weights, value_heads, preferred_element_type=j...  20.2 us
    unnamed x52, local copies, waits for them, and re-layouts  18.6 us
  transfers between devices with their start and end apart: 19, of which 13 were waited for; matrix products, arithmetic and copies ran while one was open for 23% of the time, Pallas kernels for 0%

commit v1 on v0

--- a/solution.py
+++ b/solution.py
@@ -188,10 +188,31 @@
         jnp.float32
     )
     low_grad = (rank_backward * feature_modulation).astype(jnp.bfloat16)
-    grad_rows = lax.all_gather(low_grad, "seq", axis=1, tiled=True)
+    y1 = lax.axis_size("seq")
+    u1 = lax.axis_index("seq")
+    known, upper = (y1, u1)
+    so_far_all = tuple(((u, (u - 1) % known) for u in range(known)))
+    answer = low_grad.shape[1]
+    near = low_grad
     column_partial = jnp.einsum(
-        "tc,ktr->kcr", column_block, grad_rows, preferred_element_type=jnp.float32
-    )
+        "tc,ktr->kcr",
+        lax.dynamic_slice_in_dim(column_block, upper * answer, near.shape[1], axis=0),
+        near,
+        preferred_element_type=jnp.float32,
+    )
+    m = 1
+    while m < known:
+        near = lax.ppermute(near, "seq", so_far_all)
+        now = jnp.einsum(
+            "tc,ktr->kcr",
+            lax.dynamic_slice_in_dim(
+                column_block, (upper + m) % known * answer, near.shape[1], axis=0
+            ),
+            near,
+            preferred_element_type=jnp.float32,
+        )
+        column_partial = column_partial + now
+        m = m + 1
     grad_down = lax.psum_scatter(
         column_partial.astype(jnp.bfloat16), ("cfg", "dp"), scatter_dimension=1, tiled=True
     ).astype(jnp.float32)

time: 493 us -> 509 us (1.032); the launches traced: 490 us -> 499 us
  blocking collectives: 68.7 us -> 0 us
  waiting for transfers between devices: 173 us -> 212 us
  starting transfers between devices: 65.5 us -> 103 us
    all_to_all x1 -> x0, blocking collectives: 36 us -> none  [body(): lax.all_to_all(split_view, 'seq', split_axis=2, concat_axis=0, tiled=True)]
    ppermute x0 -> x7, starting transfers between devices: none -> 33.2 us  [body(): near = lax.ppermute(near, 'seq', so_far_all)]
    all_gather x1 -> x0, blocking collectives: 32.7 us -> none  [body(): grad_rows = lax.all_gather(low_grad, 'seq', axis=1, tiled=True)]
    all_to_all x0 -> x1, waiting for transfers between devices: none -> 22 us  [body(): lax.all_to_all(split_view, 'seq', split_axis=2, concat_axis=0, tiled=True)]
    ppermute x0 -> x7, waiting for transfers between devices: none -> 15.2 us  [body(): near = lax.ppermute(near, 'seq', so_far_all)]
  transfers between devices with their start and end apart: 19 -> 27, of which waited for: 13 -> 21; matrix products, arithmetic and copies ran while one was open for 23% -> 24% of each run, Pallas kernels for 0% -> 0%
where the time goes in v1:
time: 509 us; the launch traced here: 499 us
  waiting for transfers between devices  212 us (42%)
  starting transfers between devices  103 us (20%)
  matrix products  90.1 us (18%)
  local copies, waits for them, and re-layouts  68.3 us (13%)
  between operations  16.3 us (3%)
  other arithmetic  9.83 us (2%)
    sub x8, matrix products, head_probs(): raised = jnp.exp(scores - highest)  33.6 us
    ppermute x7, starting transfers between devices, body(): near = lax.ppermute(near, 'seq', so_far_all)  33.2 us
    all_to_all x1, waiting for transfers between devices, body(): lax.all_to_all(own_pass[1], 'seq', split_axis=2, concat_axis=1, tiled=True)  22.2 us
    all_to_all x1, waiting for transfers between devices, body(): lax.all_to_all(split_view, 'seq', split_axis=2, concat_axis=0, tiled=True)  22 us
    unnamed x5, waiting for transfers between devices  21.2 us
    all_to_all x1, waiting for transfers between devices, body(): lax.all_to_all(teacher_local.astype(jnp.bfloat16), 'seq', split_axis=1, c...  21 us
    reduce_scatter x1, waiting for transfers between devices, body(): lax.psum_scatter(per_seq, ('cfg', 'dp'), scatter_dimension=1, tiled=True)  20.3 us
    dot_general x6, matrix products, one_block(): jnp.einsum('hqk,khd->qhd', weights, value_heads, preferred_element_type=j...  20.2 us
  transfers between devices with their start and end apart: 27, of which 21 were waited for; matrix products, arithmetic and copies ran while one was open for 24% of the time, Pallas kernels for 0%

profile of v1, /device:TPU:0, one launch (start us, length us, event | category | flops | bytes accessed | tf_op | source)
XLA Modules:
  0.0 499.0 jit_solution(1226713007294597672)
XLA Ops:
  11.0 7.3 %all-to-all-start.5 = ((bf16[2,128,2048]{1,0,2:T(2,128)(2,1)}), bf16[2,128,2048]{1,0,2:T(2,128)(2,1)}, u32[]{:S(2)}, u32[]{:S(2)}) async-start(bf16[2,128,2048]{1,0,2:T(2,128)(2,1)} %bitcast.333), calls=%async_computation.5 | async-start | bytes 2097152 | tf_op jit(solution)/shard_map/all_to_all | solution.py:113
  22.0 22.2 %all-to-all-done.5 = bf16[2,128,2048]{1,0,2:T(2,128)(2,1)} async-done(((bf16[2,128,2048]{1,0,2:T(2,128)(2,1)}), bf16[2,128,2048]{1,0,2:T(2,128)(2,1)}, u32[]{:S(2)}, u32[]{:S(2)}) %all-to-all-start.5) | async-done | bytes 1048608 | tf_op jit(solution)/shard_map/all_to_all | solution.py:113
  61.2 12.8 %all-to-all-done.6 = bf16[2,128,2048]{1,0,2:T(2,128)(2,1)} async-done(((bf16[2,128,2048]{1,0,2:T(2,128)(2,1)}), bf16[2,128,2048]{1,0,2:T(2,128)(2,1)}, u32[]{:S(2)}, u32[]{:S(2)}) %all-to-all-start.6) | async-done | bytes 1048608 | tf_op jit(solution)/shard_map/all_to_all | solution.py:114
  92.3 11.4 %all-to-all-done.4 = bf16[2,128,2048]{1,0,2:T(2,128)(2,1)} async-done(((bf16[2,128,2048]{1,0,2:T(2,128)(2,1)}), bf16[2,128,2048]{1,0,2:T(2,128)(2,1)}, u32[]{:S(2)}, u32[]{:S(2)}) %all-to-all-start.4) | async-done | bytes 1048608 | tf_op jit(solution)/shard_map/all_to_all | solution.py:112
  121.8 5.4 %all-to-all-start.2 = ((bf16[128,8,256]{0,2,1:T(8,128)(2,1)}), bf16[128,8,256]{0,2,1:T(8,128)(2,1)S(1)}, u32[]{:S(2)}, u32[]{:S(2)}) async-start(bf16[128,8,256]{0,2,1:T(8,128)(2,1)} %bitcast.28), calls=%async_computation.2 | async-start | bytes 1048576 | tf_op jit(solution)/shard_map/all_to_all | solution.py:163
  127.2 15.5 %while.46 = (s32[]{:T(128)}, bf16[2,512,2,128]{3,1,2,0:T(8,128)(2,1)S(1)}, bf16[2,512,2,128]{3,2,1,0:T(2,128)(2,1)S(1)}, bf16[1024,2,128]{2,0,1:T(8,128)(2,1)}, bf16[1024,2,128]{2,0,1:T(8,128)(2,1)}, /*index=5*/s32[]{:T(128)}) while((s32[]{:T(128)}, bf16[2,512,2,128]{3,1,2,0:T(8,128)(2,1)S(1)}, bf16[2,512,2,128]{3,2,1,0:T(2,128)(2,1)S(1)}, ...), condition=%wide.region_7.8_spmd, body=%wide.region_4.7_spmd.sunk | while | flops 542114816 | bytes 10756173 | solution.py:41
  147.4 6.2 %all-to-all-start = ((bf16[128,8,256]{2,0,1:T(8,128)(2,1)}), bf16[128,8,256]{2,0,1:T(8,128)(2,1)S(1)}, u32[]{:S(2)}, u32[]{:S(2)}) async-start(bf16[128,8,256]{2,0,1:T(8,128)(2,1)} %bitcast.279), calls=%async_computation | async-start | bytes 1048576 | tf_op jit(solution)/shard_map/all_to_all | solution.py:161
  154.5 16.7 %while.47 = (s32[]{:T(128)}, bf16[2,512,2,128]{3,1,2,0:T(8,128)(2,1)}, bf16[2,512,2,128]{3,2,1,0:T(2,128)(2,1)S(1)}, bf16[1024,2,128]{2,0,1:T(8,128)(2,1)}, bf16[1024,2,128]{2,0,1:T(8,128)(2,1)}, /*index=5*/s32[]{:T(128)}) while((s32[]{:T(128)}, bf16[2,512,2,128]{3,1,2,0:T(8,128)(2,1)}, bf16[2,512,2,128]{3,2,1,0:T(2,128)(2,1)S(1)}, ...), condition=%wide.region_11.12_spmd, body=%wide.region_8.11_spmd.sunk | while | flops 542114816 | bytes 10756681 | solution.py:41
  179.9 6.0 %all-to-all-start.7 = ((bf16[2,1024,256]{2,0,1:T(2,128)(2,1)}), bf16[2,1024,256]{2,0,1:T(2,128)(2,1)S(1)}, u32[]{:S(2)}, u32[]{:S(2)}) async-start(bf16[2,1024,256]{2,0,1:T(2,128)(2,1)} %copy.153), calls=%async_computation.7 | async-start | bytes 2097152 | tf_op jit(solution)/shard_map/all_to_all | solution.py:126
  189.3 21.0 %all-to-all-done.7 = bf16[2,1024,256]{2,0,1:T(2,128)(2,1)S(1)} async-done(((bf16[2,1024,256]{2,0,1:T(2,128)(2,1)}), bf16[2,1024,256]{2,0,1:T(2,128)(2,1)S(1)}, u32[]{:S(2)}, u32[]{:S(2)}) %all-to-all-start.7) | async-done | bytes 1048608 | tf_op jit(solution)/shard_map/all_to_all | solution.py:126
  215.3 13.1 %while.45 = (s32[]{:T(128)}, bf16[2,512,2,128]{3,1,2,0:T(8,128)(2,1)S(1)}, bf16[2,512,2,128]{3,1,2,0:T(8,128)(2,1)S(1)}, bf16[1024,2,128]{2,0,1:T(8,128)(2,1)S(1)}, bf16[1024,2,128]{2,0,1:T(8,128)(2,1)}, /*index=5*/s32[]{:T(128)}) while((s32[]{:T(128)}, bf16[2,512,2,128]{3,1,2,0:T(8,128)(2,1)S(1)}, bf16[2,512,2,128]{3,1,2,0:T(8,128)(2,1)S(1)}, ...), condition=%wide.region_3.4_spmd, body=%wide.region_0.3_spmd.sunk | while | flops 542114816 | bytes 12329065 | solution.py:41
  236.0 11.8 %all-to-all-done.3 = bf16[8,128,256]{2,1,0:T(8,128)(2,1)S(1)} async-done(((bf16[8,128,256]{2,1,0:T(8,128)(2,1)}), bf16[8,128,256]{2,1,0:T(8,128)(2,1)S(1)}, u32[]{:S(2)}, u32[]{:S(2)}) %all-to-all-start.3) | async-done | bytes 524320 | tf_op jit(solution)/shard_map/all_to_all | solution.py:166
  252.7 14.5 %all-to-all-done.8 = bf16[128,8,256]{2,0,1:T(8,128)(2,1)S(1)} async-done(((bf16[128,8,256]{2,0,1:T(8,128)(2,1)}), bf16[128,8,256]{2,0,1:T(8,128)(2,1)S(1)}, u32[]{:S(2)}, u32[]{:S(2)}) %all-to-all-start.8) | async-done | bytes 524320 | tf_op jit(solution)/shard_map/all_to_all | solution.py:170
  268.2 31.2 %while.48 = (s32[]{:T(128)}, f32[1024,2,128]{0,2,1:T(8,128)S(1)}, f32[1024,2,128]{0,2,1:T(8,128)}, bf16[2,512,2,128]{3,1,2,0:T(8,128)(2,1)}, bf16[2,512,2,128]{3...) while((s32[]{:T(128)}, f32[1024,2,128]{0,2,1:T(8,128)S(1)}, ...), condition=%wide.region_17.18_spmd.clone, body=%wide.region_13.17_spmd.clone.sunk | while | flops 1356201984 | bytes 79193864 | solution.py:81
  307.1 13.4 %all-to-all-done.9 = bf16[8,128,256]{2,1,0:T(8,128)(2,1)S(1)} async-done(((bf16[8,128,256]{2,1,0:T(8,128)(2,1)}), bf16[8,128,256]{2,1,0:T(8,128)(2,1)S(1)}, u32[]{:S(2)}, u32[]{:S(2)}) %all-to-all-start.9) | async-done | bytes 524320 | tf_op jit(solution)/shard_map/all_to_all | solution.py:173
  326.6 12.1 %all-to-all-done.10 = bf16[8,128,256]{2,1,0:T(8,128)(2,1)S(1)} async-done(((bf16[8,128,256]{2,1,0:T(8,128)(2,1)}), bf16[8,128,256]{2,1,0:T(8,128)(2,1)S(1)}, u32[]{:S(2)}, u32[]{:S(2)}) %all-to-all-start.10) | async-done | bytes 524320 | tf_op jit(solution)/shard_map/all_to_all | solution.py:174
  344.9 12.2 %all-to-all-done.11 = bf16[8,128,256]{2,1,0:T(8,128)(2,1)S(1)} async-done(((bf16[8,128,256]{2,1,0:T(8,128)(2,1)}), bf16[8,128,256]{2,1,0:T(8,128)(2,1)S(1)}, u32[]{:S(2)}, u32[]{:S(2)}) %all-to-all-start.11) | async-done | bytes 524320 | tf_op jit(solution)/shard_map/all_to_all | solution.py:175
  363.3 22.0 %all-to-all-done.12 = bf16[128,2,8,192]{0,3,1,2:T(8,128)(2,1)S(1)} async-done(((bf16[128,2,8,192]{0,3,1,2:T(8,128)(2,1)}), bf16[128,2,8,192]{0,3,1,2:T(8,128)(2,1)S(1)}, u32[]{:S(2)}, u32[]{:S(2)}) %all-to-all-start.12) | async-done | bytes 786464 | tf_op jit(solution)/shard_map/all_to_all | solution.py:108
  396.0 5.2 %collective-permute-start.4 = (bf16[3,128,128]{2,1,0:T(8,128)(2,1)S(1)}, bf16[3,128,128]{2,1,0:T(8,128)(2,1)S(1)}, u32[]{:S(2)}, u32[]{:S(2)}) collective-permute-start(bf16[3,128,128]{2,1,0:T(8,128)(2,1)S(1)} %collective-permute-done.3), channel_id=1, source_target_pairs={{0,14},{2,0},{4,2},{6,4},{8,6},{10,8},{12,10},{14,12},{1,15},{3,1}... | collective-permute-start | bytes 294920 | tf_op jit(solution)/shard_map/ppermute | solution.py:205
  403.4 5.1 %collective-permute-start.5 = (bf16[3,128,128]{2,1,0:T(8,128)(2,1)S(1)}, bf16[3,128,128]{2,1,0:T(8,128)(2,1)S(1)}, u32[]{:S(2)}, u32[]{:S(2)}) collective-permute-start(bf16[3,128,128]{2,1,0:T(8,128)(2,1)S(1)} %collective-permute-done.4), channel_id=1, source_target_pairs={{0,14},{2,0},{4,2},{6,4},{8,6},{10,8},{12,10},{14,12},{1,15},{3,1}... | collective-permute-start | bytes 294920 | tf_op jit(solution)/shard_map/ppermute | solution.py:205
  425.5 5.3 %collective-permute-start.8 = (bf16[3,128,128]{2,1,0:T(8,128)(2,1)S(1)}, bf16[3,128,128]{2,1,0:T(8,128)(2,1)S(1)}, u32[]{:S(2)}, u32[]{:S(2)}) collective-permute-start(bf16[3,128,128]{2,1,0:T(8,128)(2,1)S(1)} %collective-permute-done.7), channel_id=1, source_target_pairs={{0,14},{2,0},{4,2},{6,4},{8,6},{10,8},{12,10},{14,12},{1,15},{3,1}... | collective-permute-start | bytes 294920 | tf_op jit(solution)/shard_map/ppermute | solution.py:205
  434.8 5.2 %collective-permute-start.9 = (bf16[3,128,128]{2,1,0:T(8,128)(2,1)S(1)}, bf16[3,128,128]{2,1,0:T(8,128)(2,1)S(1)}, u32[]{:S(2)}, u32[]{:S(2)}) collective-permute-start(bf16[3,128,128]{2,1,0:T(8,128)(2,1)S(1)} %collective-permute-done.8), channel_id=1, source_target_pairs={{0,14},{2,0},{4,2},{6,4},{8,6},{10,8},{12,10},{14,12},{1,15},{3,1}... | collective-permute-start | bytes 294920 | tf_op jit(solution)/shard_map/ppermute | solution.py:205
  447.9 20.6 %reduce-scatter.13.cloned.1.call-done = bf16[96,384]{1,0:T(8,128)(2,1)} async-done(((bf16[384,384]{1,0:T(8,128)(2,1)}), bf16[96,384]{1,0:T(8,128)(2,1)}) %reduce-scatter.13.cloned.1.call-update) | async-done | bytes 73744
  470.4 20.3 %reduce-scatter.11.cloned.1.call-done = bf16[3,32,256]{2,1,0:T(8,128)(2,1)} async-done(((bf16[3,128,256]{2,1,0:T(8,128)(2,1)}), bf16[3,32,256]{2,1,0:T(8,128)(2,1)}) %reduce-scatter.11.cloned.1.call-update) | async-done | bytes 49168 | tf_op jit(solution)/shard_map/reduce_scatter | solution.py:187
  (232 shorter events, 242.7 us)
Async XLA Ops:
  11.0 33.2 %all-to-all-start.5 = ((bf16[2,128,2048]{1,0,2:T(2,128)(2,1)}), bf16[2,128,2048]{1,0,2:T(2,128)(2,1)}, u32[]{:S(2)}, u32[]{:S(2)}) async-start(bf16[2,128,2048]{1,0,2:T(2,128)(2,1)} %bitcast.333), calls=%async_computation.5 | async-start | bytes 2097152 | tf_op jit(solution)/shard_map/all_to_all | solution.py:113
  44.2 29.8 %all-to-all-start.6 = ((bf16[2,128,2048]{1,0,2:T(2,128)(2,1)}), bf16[2,128,2048]{1,0,2:T(2,128)(2,1)}, u32[]{:S(2)}, u32[]{:S(2)}) async-start(bf16[2,128,2048]{1,0,2:T(2,128)(2,1)} %bitcast.332), calls=%async_computation.6 | async-start | bytes 2097152 | tf_op jit(solution)/shard_map/all_to_all | solution.py:114
  49.3 39.0 %collective-permute-start.1 = (bf16[128,2048]{1,0:T(8,128)(2,1)}, bf16[128,2048]{1,0:T(8,128)(2,1)}, u32[]{:S(2)}, u32[]{:S(2)}) collective-permute-start(bf16[128,2048]{1,0:T(8,128)(2,1)} %slice_bitcast_fusion.1), channel_id=1, source_target_pairs={{0,16},{1,17},{2,18},{3,19},{4,20},{5,21},{6,22},{7,23},{8,24},{9,... | collective-permute-start | bytes 1572872 | tf_op jit(solution)/shard_map/ppermute | solution.py:15
  55.4 35.4 %collective-permute-start.2 = (bf16[128,2048]{1,0:T(8,128)(2,1)}, bf16[128,2048]{1,0:T(8,128)(2,1)}, u32[]{:S(2)}, u32[]{:S(2)}) collective-permute-start(bf16[128,2048]{1,0:T(8,128)(2,1)} %slice_bitcast_fusion), channel_id=1, source_target_pairs={{0,16},{1,17},{2,18},{3,19},{4,20},{5,21},{6,22},{7,23},{8,24},{9,... | collective-permute-start | bytes 1572872 | tf_op jit(solution)/shard_map/ppermute | solution.py:15
  74.0 29.7 %all-to-all-start.4 = ((bf16[2,128,2048]{1,0,2:T(2,128)(2,1)}), bf16[2,128,2048]{1,0,2:T(2,128)(2,1)}, u32[]{:S(2)}, u32[]{:S(2)}) async-start(bf16[2,128,2048]{1,0,2:T(2,128)(2,1)} %bitcast.331), calls=%async_computation.4 | async-start | bytes 2097152 | tf_op jit(solution)/shard_map/all_to_all | solution.py:112
  80.2 27.1 %collective-permute-start = (bf16[128,2048]{1,0:T(8,128)(2,1)}, bf16[128,2048]{1,0:T(8,128)(2,1)}, u32[]{:S(2)}, u32[]{:S(2)}) collective-permute-start(bf16[128,2048]{1,0:T(8,128)(2,1)} %slice_bitcast_fusion.2), channel_id=1, source_target_pairs={{0,16},{1,17},{2,18},{3,19},{4,20},{5,21},{6,22},{7,23},{8,24},{9,... | collective-permute-start | bytes 1572872 | tf_op jit(solution)/shard_map/ppermute | solution.py:15
  103.7 18.0 %all-to-all-start.1 = ((bf16[128,8,256]{0,2,1:T(8,128)(2,1)}), bf16[128,8,256]{0,2,1:T(8,128)(2,1)S(1)}, u32[]{:S(2)}, u32[]{:S(2)}) async-start(bf16[128,8,256]{0,2,1:T(8,128)(2,1)} %bitcast.22), calls=%async_computation.1 | async-start | bytes 1048576 | tf_op jit(solution)/shard_map/all_to_all | solution.py:162
  121.8 25.7 %all-to-all-start.2 = ((bf16[128,8,256]{0,2,1:T(8,128)(2,1)}), bf16[128,8,256]{0,2,1:T(8,128)(2,1)S(1)}, u32[]{:S(2)}, u32[]{:S(2)}) async-start(bf16[128,8,256]{0,2,1:T(8,128)(2,1)} %bitcast.28), calls=%async_computation.2 | async-start | bytes 1048576 | tf_op jit(solution)/shard_map/all_to_all | solution.py:163
  147.4 31.6 %all-to-all-start = ((bf16[128,8,256]{2,0,1:T(8,128)(2,1)}), bf16[128,8,256]{2,0,1:T(8,128)(2,1)S(1)}, u32[]{:S(2)}, u32[]{:S(2)}) async-start(bf16[128,8,256]{2,0,1:T(8,128)(2,1)} %bitcast.279), calls=%async_computation | async-start | bytes 1048576 | tf_op jit(solution)/shard_map/all_to_all | solution.py:161
  179.9 30.4 %all-to-all-start.7 = ((bf16[2,1024,256]{2,0,1:T(2,128)(2,1)}), bf16[2,1024,256]{2,0,1:T(2,128)(2,1)S(1)}, u32[]{:S(2)}, u32[]{:S(2)}) async-start(bf16[2,1024,256]{2,0,1:T(2,128)(2,1)} %copy.153), calls=%async_computation.7 | async-start | bytes 2097152 | tf_op jit(solution)/shard_map/all_to_all | solution.py:126
  185.8 48.9 %reduce-scatter.7.cloned.1.call-start = ((), (), s32[]{:S(2)}) async-start(), calls=%async_computation.17 | async-start | bytes 1572864 | tf_op jit(solution)/shard_map/reduce_scatter | solution.py:135
  230.1 17.7 %all-to-all-start.3 = ((bf16[8,128,256]{2,1,0:T(8,128)(2,1)}), bf16[8,128,256]{2,1,0:T(8,128)(2,1)S(1)}, u32[]{:S(2)}, u32[]{:S(2)}) async-start(bf16[8,128,256]{2,1,0:T(8,128)(2,1)} %convert_element_type.140), calls=%async_computation.3 | async-start | bytes 1048576 | tf_op jit(solution)/shard_map/all_to_all | solution.py:166
  248.8 18.3 %all-to-all-start.8 = ((bf16[128,8,256]{2,0,1:T(8,128)(2,1)}), bf16[128,8,256]{2,0,1:T(8,128)(2,1)S(1)}, u32[]{:S(2)}, u32[]{:S(2)}) async-start(bf16[128,8,256]{2,0,1:T(8,128)(2,1)} %multiply_convert_fusion.1), calls=%async_computation.9 | async-start | bytes 1048576 | tf_op jit(solution)/shard_map/all_to_all | solution.py:170
  302.1 18.3 %all-to-all-start.9 = ((bf16[8,128,256]{2,1,0:T(8,128)(2,1)}), bf16[8,128,256]{2,1,0:T(8,128)(2,1)S(1)}, u32[]{:S(2)}, u32[]{:S(2)}) async-start(bf16[8,128,256]{2,1,0:T(8,128)(2,1)} %convert_element_type.149), calls=%async_computation.10 | async-start | bytes 1048576 | tf_op jit(solution)/shard_map/all_to_all | solution.py:173
  320.4 18.3 %all-to-all-start.10 = ((bf16[8,128,256]{2,1,0:T(8,128)(2,1)}), bf16[8,128,256]{2,1,0:T(8,128)(2,1)S(1)}, u32[]{:S(2)}, u32[]{:S(2)}) async-start(bf16[8,128,256]{2,1,0:T(8,128)(2,1)} %copy.201), calls=%async_computation.11 | async-start | bytes 1048576 | tf_op jit(solution)/shard_map/all_to_all | solution.py:174
  338.8 18.3 %all-to-all-start.11 = ((bf16[8,128,256]{2,1,0:T(8,128)(2,1)}), bf16[8,128,256]{2,1,0:T(8,128)(2,1)S(1)}, u32[]{:S(2)}, u32[]{:S(2)}) async-start(bf16[8,128,256]{2,1,0:T(8,128)(2,1)} %copy.202), calls=%async_computation.12 | async-start | bytes 1048576 | tf_op jit(solution)/shard_map/all_to_all | solution.py:175
  357.1 28.3 %all-to-all-start.12 = ((bf16[128,2,8,192]{0,3,1,2:T(8,128)(2,1)}), bf16[128,2,8,192]{0,3,1,2:T(8,128)(2,1)S(1)}, u32[]{:S(2)}, u32[]{:S(2)}) async-start(bf16[128,2,8,192]{0,3,1,2:T(8,128)(2,1)} %copy.168), calls=%async_computation.13 | async-start | bytes 1572864 | tf_op jit(solution)/shard_map/all_to_all | solution.py:108
  360.7 85.4 %reduce-scatter.9.cloned.1.call-start = ((), (), s32[]{:S(2)}) async-start(), calls=%async_computation.18 | async-start | bytes 1769472 | tf_op jit(solution)/shard_map/reduce_scatter | solution.py:184
  363.2 105.4 %reduce-scatter.13.cloned.1.call-start = ((), (), s32[]{:S(2)}) async-start(), calls=%async_computation.20 | async-start | bytes 368640
  396.0 7.4 %collective-permute-start.4 = (bf16[3,128,128]{2,1,0:T(8,128)(2,1)S(1)}, bf16[3,128,128]{2,1,0:T(8,128)(2,1)S(1)}, u32[]{:S(2)}, u32[]{:S(2)}) collective-permute-start(bf16[3,128,128]{2,1,0:T(8,128)(2,1)S(1)} %collective-permute-done.3), channel_id=1, source_target_pairs={{0,14},{2,0},{4,2},{6,4},{8,6},{10,8},{12,10},{14,12},{1,15},{3,1}... | collective-permute-start | bytes 294920 | tf_op jit(solution)/shard_map/ppermute | solution.py:205
  418.0 7.4 %collective-permute-start.7 = (bf16[3,128,128]{2,1,0:T(8,128)(2,1)S(1)}, bf16[3,128,128]{2,1,0:T(8,128)(2,1)S(1)}, u32[]{:S(2)}, u32[]{:S(2)}) collective-permute-start(bf16[3,128,128]{2,1,0:T(8,128)(2,1)S(1)} %collective-permute-done.6), channel_id=1, source_target_pairs={{0,14},{2,0},{4,2},{6,4},{8,6},{10,8},{12,10},{14,12},{1,15},{3,1}... | collective-permute-start | bytes 294920 | tf_op jit(solution)/shard_map/ppermute | solution.py:205
  425.5 9.3 %collective-permute-start.8 = (bf16[3,128,128]{2,1,0:T(8,128)(2,1)S(1)}, bf16[3,128,128]{2,1,0:T(8,128)(2,1)S(1)}, u32[]{:S(2)}, u32[]{:S(2)}) collective-permute-start(bf16[3,128,128]{2,1,0:T(8,128)(2,1)S(1)} %collective-permute-done.7), channel_id=1, source_target_pairs={{0,14},{2,0},{4,2},{6,4},{8,6},{10,8},{12,10},{14,12},{1,15},{3,1}... | collective-permute-start | bytes 294920 | tf_op jit(solution)/shard_map/ppermute | solution.py:205
  434.8 7.4 %collective-permute-start.9 = (bf16[3,128,128]{2,1,0:T(8,128)(2,1)S(1)}, bf16[3,128,128]{2,1,0:T(8,128)(2,1)S(1)}, u32[]{:S(2)}, u32[]{:S(2)}) collective-permute-start(bf16[3,128,128]{2,1,0:T(8,128)(2,1)S(1)} %collective-permute-done.8), channel_id=1, source_target_pairs={{0,14},{2,0},{4,2},{6,4},{8,6},{10,8},{12,10},{14,12},{1,15},{3,1}... | collective-permute-start | bytes 294920 | tf_op jit(solution)/shard_map/ppermute | solution.py:205
  446.1 44.6 %reduce-scatter.11.cloned.1.call-start = ((), (), s32[]{:S(2)}) async-start(), calls=%async_computation.19 | async-start | bytes 245760 | tf_op jit(solution)/shard_map/reduce_scatter | solution.py:187
  (34 other events, 603.5 us)
Sparse Core Ops, SparseCore 0:
  215.3 19.3 reduce-scatter.6
  365.0 71.8 reduce-scatter.8
  446.2 22.3 reduce-scatter.12
  470.9 19.7 reduce-scatter.10
